TPU v7x, 128 devices: a whole 4x4x4 slice. The times are simulated.
128 devices in a mesh: gx: 16 (over x, z), gy: 8 (over y, core).
Axes of the slice: x: 4, y: 4, z: 4, core: 2. Of those that a mesh axis runs over, the one named last changes fastest.
Arguments:
- source_tiles: bfloat16 [384, 32, 192, 384], P(('gx', 'gy')), may hold values from -6 to 6
- tile_offsets: int32 [2, 384], P(None, ('gx', 'gy')), may hold values from -128 to 1920, as said below
- tile_shifts: int32 [384], P(('gx', 'gy')), may hold values from 0 to 63
- tile_counts: int32 [128], P(('gx', 'gy')), may hold values from 1 to 3, as said below
Outputs:
- merged_slab: float32 [32, 2048, 2048], P(None, 'gx', 'gy')
Inputs may be any that keep to these rules, and one draw needn't show every extreme that they name: `tile_offsets`: slot k belongs to the device of joined gx+gy index d = k // 3, that is gx index d // 8 and gy index d % 8. Its x offset lies from that gx index times 128 minus 64 up to that gx index times 128; its y offset from the gy index times 256 minus 128 up to the gy index times 256. So every tile covers its owner's whole block. `tile_counts`: entry d counts the used slots of device d; they are its first slots, the others are ignored. Both 1 and 3 occur in every draw.
All inputs are finite; a program needn't handle non-finite values.
Results may differ from a plain program's by a relative error of at most 0.0003.
Values sent between devices are 32-bit elements; how exact they have to be, the bound alone decides.
A program may use at most 192 MiB of HBM per device.

v0:
```python
import jax
import jax.numpy as jnp
from jax import lax
from jax.experimental import pallas as pl
from jax.experimental.pallas import tpu as pltpu
from jax.sharding import PartitionSpec as P

NZ = 32
BX = 128
BY = 256
TX = 192
TY = 384
CAP = 3
RAMP = 32
RX = 64
RY = 128
WX = BX + 2 * RX
WY = BY + 2 * RY
SLOTS = NZ + 1
LAG_Y = 2
LAG_X = 4
ROWS = 16
MESH = pl.DeviceIdType.MESH


def ramp(places, length):
    return jnp.minimum(jnp.minimum(places + 1, length - places), RAMP)


def taps(places, length, fraction):
    inside = (places >= 0) & (places < length)
    blend = jnp.where(inside, ramp(places, length), 0).astype(jnp.float32)
    last = jnp.where(places == length - 1, fraction, 0.0)
    return blend, blend * (1.0 - fraction + last), blend * fraction


def kernel(
    tiles, offsets, shifts, counts, out,
    source, edge_low, edge_high, block, from_low, from_high, from_left, from_right,
    mid, split, spread_y, spread_x, inverse,
    load_sem, store_sem, send_low, send_high, send_left, send_right,
    recv_low, recv_high, recv_left, recv_right,
):
    gx = lax.axis_index("gx")
    gy = lax.axis_index("gy")
    last_x = lax.axis_size("gx") - 1
    last_y = lax.axis_size("gy") - 1
    has_low, has_high = gy > 0, gy < last_y
    has_left, has_right = gx > 0, gx < last_x

    def load(z):
        return pltpu.make_async_copy(tiles.at[:, z], source.at[:, z], load_sem.at[z])

    def store(z):
        return pltpu.make_async_copy(
            block.at[z + 1, pl.ds(RX, BX)], out.at[z], store_sem.at[z]
        )

    def to_low(slot):
        return pltpu.make_async_remote_copy(
            src_ref=edge_low.at[slot], dst_ref=from_high.at[slot],
            send_sem=send_low.at[slot], recv_sem=recv_high.at[slot],
            device_id={"gy": gy - 1}, device_id_type=MESH,
        )

    def to_high(slot):
        return pltpu.make_async_remote_copy(
            src_ref=edge_high.at[slot], dst_ref=from_low.at[slot],
            send_sem=send_high.at[slot], recv_sem=recv_low.at[slot],
            device_id={"gy": gy + 1}, device_id_type=MESH,
        )

    def to_left(slot):
        return pltpu.make_async_remote_copy(
            src_ref=block.at[slot, pl.ds(0, RX)], dst_ref=from_right.at[slot],
            send_sem=send_left.at[slot], recv_sem=recv_right.at[slot],
            device_id={"gx": gx - 1}, device_id_type=MESH,
        )

    def to_right(slot):
        return pltpu.make_async_remote_copy(
            src_ref=block.at[slot, pl.ds(RX + BX, RX)], dst_ref=from_left.at[slot],
            send_sem=send_right.at[slot], recv_sem=recv_left.at[slot],
            device_id={"gx": gx + 1}, device_id_type=MESH,
        )

    load(0).start()
    load(1).start()

    barrier = pltpu.get_barrier_semaphore()
    for present, place in (
        (has_low, {"gy": gy - 1}), (has_high, {"gy": gy + 1}),
        (has_left, {"gx": gx - 1}), (has_right, {"gx": gx + 1}),
    ):
        @pl.when(present)
        def _(place=place):
            pl.semaphore_signal(barrier, inc=1, device_id=place, device_id_type=MESH)

    def start_y(slot):
        @pl.when(has_low)
        def _():
            to_low(slot).start()

        @pl.when(has_high)
        def _():
            to_high(slot).start()

    starts_x, starts_y, parts, used = [], [], [], []
    for k in range(CAP):
        code = shifts[k]
        starts_x.append(offsets[0, k] - gx * BX + RX)
        starts_y.append(offsets[1, k] - gy * BY + RY)
        parts.append([
            ((code >> bits) & 3).astype(jnp.float32) * 0.25 for bits in (4, 2, 0)
        ])
        used.append(jnp.where(k < counts[0], 1.0, 0.0).astype(jnp.float32))

    rows_x = lax.broadcasted_iota(jnp.int32, (WX, 128), 0)
    cells_y = lax.broadcasted_iota(jnp.int32, (8, WY), 1)
    plane_y, taps_y, total = [], [], []
    for k in range(CAP):
        taps_y.append(taps(cells_y - starts_y[k], TY, parts[k][2]))
    for n in range(WY // 128):
        total = jnp.zeros((WX, 128), jnp.float32)
        for k in range(CAP):
            blend_x = taps(rows_x - starts_x[k], TX, parts[k][1])[0] * used[k]
            total = total + blend_x * taps_y[k][0][0:1, n * 128 : (n + 1) * 128]
        if n == 0:
            edge_low[0] = total
        elif n == WY // 128 - 1:
            edge_high[0] = total
        else:
            block[0, :, (n - 1) * 128 : n * 128] = total

    pl.semaphore_wait(
        barrier,
        has_low.astype(jnp.int32) + has_high.astype(jnp.int32)
        + has_left.astype(jnp.int32) + has_right.astype(jnp.int32),
    )
    start_y(0)

    def start_load(z, carry):
        load(z).start()
        return carry

    lax.fori_loop(2, NZ, start_load, 0)

    for k in range(CAP):
        for r in range(0, TY, 64):
            apart = (
                lax.broadcasted_iota(jnp.int32, (64, WY), 0) + r
                - lax.broadcasted_iota(jnp.int32, (64, WY), 1) + starts_y[k]
            )
            here, after = taps_y[k][1][0:1], taps_y[k][2][0:1]
            spread_y[k, r : r + 64] = jnp.where(
                apart == 0, here, jnp.where(apart == 1, after, 0.0)
            ).astype(jnp.bfloat16)
        lane = lax.broadcasted_iota(jnp.int32, (64, 2 * TX), 1)
        lane = jnp.where(lane >= TX, lane - TX, lane)
        for r in range(0, WX, 64):
            place = lax.broadcasted_iota(jnp.int32, (64, 2 * TX), 0) + r - starts_x[k]
            _, here, after = taps(place, TX, parts[k][1])
            apart = lane - place
            spread_x[r : r + 64, k * 2 * TX : (k + 1) * 2 * TX] = (
                jnp.where(apart == 0, here, jnp.where(apart == 1, after, 0.0)) * used[k]
            ).astype(jnp.bfloat16)

    def along_y(z):
        load(z).wait()
        for k in range(CAP):
            mid[z % 2, k] = jnp.dot(
                source[k, z], spread_y[k], preferred_element_type=jnp.float32
            )

    along_y(0)

    def step(slot, carry):
        @pl.when(slot < SLOTS)
        def _():
            z = slot - 1

            @pl.when(z < NZ - 1)
            def _():
                along_y(z + 1)

            now = z % 2
            then = jnp.minimum(z + 1, NZ - 1) % 2
            for k in range(CAP):
                depth_part = parts[k][0]
                for r in range(0, TX, ROWS):
                    volume = (1.0 - depth_part) * mid[now, k, r : r + ROWS] + (
                        depth_part * mid[then, k, r : r + ROWS]
                    )
                    coarse = volume.astype(jnp.bfloat16)
                    fine = (volume - coarse.astype(jnp.float32)).astype(jnp.bfloat16)
                    split[k * 2 * TX + r : k * 2 * TX + r + ROWS] = coarse
                    split[k * 2 * TX + TX + r : k * 2 * TX + TX + r + ROWS] = fine
            for n in range(2):
                piece = jnp.dot(
                    spread_x[...], split[:, n * 256 : (n + 1) * 256],
                    preferred_element_type=jnp.float32,
                )
                if n == 0:
                    edge_low[slot] = piece[:, :128]
                    block[slot, :, :128] = piece[:, 128:]
                else:
                    block[slot, :, 128:] = piece[:, :128]
                    edge_high[slot] = piece[:, 128:]
            start_y(slot)

        ready = slot - LAG_Y

        @pl.when((ready >= 0) & (ready < SLOTS))
        def _():
            @pl.when(has_low)
            def _():
                to_high(ready).wait_recv()
                block[ready, :, :RY] += from_low[ready]

            @pl.when(has_high)
            def _():
                to_low(ready).wait_recv()
                block[ready, :, RY:] += from_high[ready]

            @pl.when(has_left)
            def _():
                to_left(ready).start()

            @pl.when(has_right)
            def _():
                to_right(ready).start()

        done = slot - LAG_X

        @pl.when((done >= 0) & (done < SLOTS))
        def _():
            @pl.when(has_left)
            def _():
                to_right(done).wait_recv()
                block[done, RX : 2 * RX] += from_left[done]

            @pl.when(has_right)
            def _():
                to_left(done).wait_recv()
                block[done, 2 * RX : 3 * RX] += from_right[done]

            @pl.when(done == 0)
            def _():
                inverse[...] = 1.0 / jnp.maximum(block[0, RX : RX + BX], 1.0)

            @pl.when(done > 0)
            def _():
                block[done, RX : RX + BX] *= inverse[...]
                store(done - 1).start()

        return carry

    lax.fori_loop(1, SLOTS + LAG_X, step, 0)

    def finish(slot, carry):
        @pl.when(has_low)
        def _():
            to_low(slot).wait_send()

        @pl.when(has_high)
        def _():
            to_high(slot).wait_send()

        @pl.when(has_left)
        def _():
            to_left(slot).wait_send()

        @pl.when(has_right)
        def _():
            to_right(slot).wait_send()

        @pl.when(slot < NZ)
        def _():
            store(slot).wait()

        return carry

    lax.fori_loop(0, SLOTS, finish, 0)


def local(source_tiles, tile_offsets, tile_shifts, tile_counts):
    hbm = pl.BlockSpec(memory_space=pl.ANY)
    smem = pl.BlockSpec(memory_space=pltpu.SMEM)
    dma = pltpu.SemaphoreType.DMA
    return pl.pallas_call(
        kernel,
        out_shape=jax.ShapeDtypeStruct((NZ, BX, BY), jnp.float32),
        in_specs=[hbm, smem, smem, smem],
        out_specs=hbm,
        scratch_shapes=[
            pltpu.VMEM((CAP, NZ, TX, TY), jnp.bfloat16),
            pltpu.VMEM((SLOTS, WX, RY), jnp.float32),
            pltpu.VMEM((SLOTS, WX, RY), jnp.float32),
            pltpu.VMEM((SLOTS, WX, BY), jnp.float32),
            pltpu.VMEM((SLOTS, WX, RY), jnp.float32),
            pltpu.VMEM((SLOTS, WX, RY), jnp.float32),
            pltpu.VMEM((SLOTS, RX, BY), jnp.float32),
            pltpu.VMEM((SLOTS, RX, BY), jnp.float32),
            pltpu.VMEM((2, CAP, TX, WY), jnp.float32),
            pltpu.VMEM((CAP * 2 * TX, WY), jnp.bfloat16),
            pltpu.VMEM((CAP, TY, WY), jnp.bfloat16),
            pltpu.VMEM((WX, CAP * 2 * TX), jnp.bfloat16),
            pltpu.VMEM((BX, BY), jnp.float32),
            dma((NZ,)), dma((NZ,)),
            dma((SLOTS,)), dma((SLOTS,)), dma((SLOTS,)), dma((SLOTS,)),
            dma((SLOTS,)), dma((SLOTS,)), dma((SLOTS,)), dma((SLOTS,)),
        ],
        compiler_params=pltpu.CompilerParams(
            collective_id=0, has_side_effects=True, vmem_limit_bytes=62 * 1024 * 1024,
        ),
    )(source_tiles, tile_offsets, tile_shifts, tile_counts)


def solution(mesh):
    placed = (
        P(("gx", "gy"), None, None, None),
        P(None, ("gx", "gy")),
        P(("gx", "gy")),
        P(("gx", "gy")),
    )
    return jax.shard_map(
        local, mesh=mesh, in_specs=placed, out_specs=P(None, "gx", "gy"), check_vma=False
    )
```

profile of v0, /device:TPU:15, one launch (start us, length us, event | category | flops | bytes accessed | tf_op | source)
XLA Modules:
  0.0 82.4 jit_solution(15145613056486208413)
XLA Ops:
  0.7 77.1 %shard_map.46 = f32[32,128,256]{2,1,0:T(8,128)} custom-call(bf16[3,32,192,384]{3,2,1,0:T(8,128)(2,1)} %tiles.1, s32[2,3]{1,0:T(2,128)} %offsets.1, s32[3]{0:T(128)} %shifts.1, s32[1]{0:T(128)S(6)} %copy.6.counts), custom_call_target="tpu_custom_call" | custom-call | tf_op jit(solution)/shard_map/pallas_call | solution.py:290
  77.7 4.7 %copy.7 = f32[32,128,256]{2,1,0:T(8,128)} copy(f32[32,128,256]{2,1,0:T(8,128)} %shard_map.46) | data formatting | bytes 8388608
where the time goes:
time: 82.7 us; the launch traced here: 82.4 us
  Pallas kernels  77.1 us (93%)
  local copies, waits for them, and re-layouts  4.66 us (6%)
    pallas_call x1, Pallas kernels, local(): pl.pallas_call(kernel, out_shape=jax.ShapeDtypeStruct((NZ, BX, BY), jnp.f...  77.1 us
    unnamed x1, local copies, waits for them, and re-layouts  4.66 us

commit v1 on v0

--- a/solution.py
+++ b/solution.py
@@ -16,9 +16,9 @@
 RY = 128
 WX = BX + 2 * RX
 WY = BY + 2 * RY
-SLOTS = NZ + 1
-LAG_Y = 2
-LAG_X = 4
+SLOTS = NZ
+LAG_Y = 3
+LAG_X = 8
 ROWS = 16
 MESH = pl.DeviceIdType.MESH
 
@@ -38,7 +38,8 @@
     tiles, offsets, shifts, counts, out,
     source, edge_low, edge_high, block, from_low, from_high, from_left, from_right,
     mid, split, spread_y, spread_x, inverse,
-    load_sem, store_sem, send_low, send_high, send_left, send_right,
+    ramps, ramps_from_low, ramps_from_high, around, around_left, around_right,
+    load_sem, ramp_sem, send_low, send_high, send_left, send_right,
     recv_low, recv_high, recv_left, recv_right,
 ):
     gx = lax.axis_index("gx")
@@ -51,11 +52,6 @@
     def load(z):
         return pltpu.make_async_copy(tiles.at[:, z], source.at[:, z], load_sem.at[z])
 
-    def store(z):
-        return pltpu.make_async_copy(
-            block.at[z + 1, pl.ds(RX, BX)], out.at[z], store_sem.at[z]
-        )
-
     def to_low(slot):
         return pltpu.make_async_remote_copy(
             src_ref=edge_low.at[slot], dst_ref=from_high.at[slot],
@@ -84,8 +80,36 @@
             device_id={"gx": gx + 1}, device_id_type=MESH,
         )
 
-    load(0).start()
-    load(1).start()
+    def ramps_low():
+        return pltpu.make_async_remote_copy(
+            src_ref=ramps, dst_ref=ramps_from_high,
+            send_sem=ramp_sem.at[0], recv_sem=ramp_sem.at[4],
+            device_id={"gy": gy - 1}, device_id_type=MESH,
+        )
+
+    def ramps_high():
+        return pltpu.make_async_remote_copy(
+            src_ref=ramps, dst_ref=ramps_from_low,
+            send_sem=ramp_sem.at[1], recv_sem=ramp_sem.at[5],
+            device_id={"gy": gy + 1}, device_id_type=MESH,
+        )
+
+    def ramps_left():
+        return pltpu.make_async_remote_copy(
+            src_ref=around, dst_ref=around_right,
+            send_sem=ramp_sem.at[2], recv_sem=ramp_sem.at[6],
+            device_id={"gx": gx - 1}, device_id_type=MESH,
+        )
+
+    def ramps_right():
+        return pltpu.make_async_remote_copy(
+            src_ref=around, dst_ref=around_left,
+            send_sem=ramp_sem.at[3], recv_sem=ramp_sem.at[7],
+            device_id={"gx": gx + 1}, device_id_type=MESH,
+        )
+
+    for z in range(4):
+        load(z).start()
 
     barrier = pltpu.get_barrier_semaphore()
     for present, place in (
@@ -115,35 +139,24 @@
         ])
         used.append(jnp.where(k < counts[0], 1.0, 0.0).astype(jnp.float32))
 
-    rows_x = lax.broadcasted_iota(jnp.int32, (WX, 128), 0)
-    cells_y = lax.broadcasted_iota(jnp.int32, (8, WY), 1)
-    plane_y, taps_y, total = [], [], []
+    taps_y = [
+        taps(lax.broadcasted_iota(jnp.int32, (8, WY), 1) - starts_y[k], TY, parts[k][2])
+        for k in range(CAP)
+    ]
+    taps_x = [
+        taps(lax.broadcasted_iota(jnp.int32, (8, WX), 1) - starts_x[k], TX, parts[k][1])
+        for k in range(CAP)
+    ]
+    ramps[...] = jnp.zeros_like(ramps)
     for k in range(CAP):
-        taps_y.append(taps(cells_y - starts_y[k], TY, parts[k][2]))
-    for n in range(WY // 128):
-        total = jnp.zeros((WX, 128), jnp.float32)
-        for k in range(CAP):
-            blend_x = taps(rows_x - starts_x[k], TX, parts[k][1])[0] * used[k]
-            total = total + blend_x * taps_y[k][0][0:1, n * 128 : (n + 1) * 128]
-        if n == 0:
-            edge_low[0] = total
-        elif n == WY // 128 - 1:
-            edge_high[0] = total
-        else:
-            block[0, :, (n - 1) * 128 : n * 128] = total
-
-    pl.semaphore_wait(
-        barrier,
-        has_low.astype(jnp.int32) + has_high.astype(jnp.int32)
-        + has_left.astype(jnp.int32) + has_right.astype(jnp.int32),
-    )
-    start_y(0)
+        ramps[k : k + 1, :WX] = taps_x[k][0][0:1] * used[k]
+        ramps[k : k + 1, WX:] = taps_y[k][0][0:1]
 
     def start_load(z, carry):
         load(z).start()
         return carry
 
-    lax.fori_loop(2, NZ, start_load, 0)
+    lax.fori_loop(4, NZ, start_load, 0)
 
     for k in range(CAP):
         for r in range(0, TY, 64):
@@ -172,41 +185,111 @@
                 source[k, z], spread_y[k], preferred_element_type=jnp.float32
             )
 
+    def resample_x(z):
+        now = z % 2
+        then = jnp.minimum(z + 1, NZ - 1) % 2
+        for k in range(CAP):
+            depth_part = parts[k][0]
+            for r in range(0, TX, ROWS):
+                volume = (1.0 - depth_part) * mid[now, k, r : r + ROWS] + (
+                    depth_part * mid[then, k, r : r + ROWS]
+                )
+                coarse = volume.astype(jnp.bfloat16)
+                fine = (volume - coarse.astype(jnp.float32)).astype(jnp.bfloat16)
+                split[k * 2 * TX + r : k * 2 * TX + r + ROWS] = coarse
+                split[k * 2 * TX + TX + r : k * 2 * TX + TX + r + ROWS] = fine
+        for n in range(2):
+            piece = jnp.dot(
+                spread_x[...], split[:, n * 256 : (n + 1) * 256],
+                preferred_element_type=jnp.float32,
+            )
+            if n == 0:
+                edge_low[z] = piece[:, :128]
+                block[z, :, :128] = piece[:, 128:]
+            else:
+                block[z, :, 128:] = piece[:, :128]
+                edge_high[z] = piece[:, 128:]
+
     along_y(0)
+    along_y(1)
+    resample_x(0)
+
+    pl.semaphore_wait(
+        barrier,
+        has_low.astype(jnp.int32) + has_high.astype(jnp.int32)
+        + has_left.astype(jnp.int32) + has_right.astype(jnp.int32),
+    )
+    start_y(0)
+
+    @pl.when(has_low)
+    def _():
+        ramps_low().start()
+
+    @pl.when(has_high)
+    def _():
+        ramps_high().start()
+
+    def gather_ramps():
+        around[...] = jnp.zeros_like(around)
+        around[0:8, :WX] = ramps[:, :WX]
+        around[0:8, WX:] = ramps[:, WX + RY : WX + RY + BY]
+
+        @pl.when(has_low)
+        def _():
+            ramps_high().wait_recv()
+            around[8:16, :WX] = ramps_from_low[:, :WX]
+            around[8:16, WX : WX + RY] = ramps_from_low[:, WX + RY + BY :]
+
+        @pl.when(has_high)
+        def _():
+            ramps_low().wait_recv()
+            around[16:24, :WX] = ramps_from_high[:, :WX]
+            around[16:24, WX + RY :] = ramps_from_high[:, WX : WX + RY]
+
+        @pl.when(has_left)
+        def _():
+            ramps_left().start()
+
+        @pl.when(has_right)
+        def _():
+            ramps_right().start()
+
+    def weights(rows):
+        return lax.dot_general(
+            rows[:, :WX].astype(jnp.bfloat16), rows[:, WX:].astype(jnp.bfloat16),
+            (((0,), (0,)), ((), ())), preferred_element_type=jnp.float32,
+        )
+
+    def invert():
+        inverse[...] = weights(around[...])[RX : RX + BX]
+
+        @pl.when(has_left)
+        def _():
+            ramps_right().wait_recv()
+            inverse[:RX] += weights(around_left[...])[RX + BX :]
+
+        @pl.when(has_right)
+        def _():
+            ramps_left().wait_recv()
+            inverse[RX:] += weights(around_right[...])[:RX]
+
+        inverse[...] = 1.0 / jnp.maximum(inverse[...], 1.0)
 
     def step(slot, carry):
         @pl.when(slot < SLOTS)
         def _():
-            z = slot - 1
+            z = slot
 
             @pl.when(z < NZ - 1)
             def _():
                 along_y(z + 1)
 
-            now = z % 2
-            then = jnp.minimum(z + 1, NZ - 1) % 2
-            for k in range(CAP):
-                depth_part = parts[k][0]
-                for r in range(0, TX, ROWS):
-                    volume = (1.0 - depth_part) * mid[now, k, r : r + ROWS] + (
-                        depth_part * mid[then, k, r : r + ROWS]
-                    )
-                    coarse = volume.astype(jnp.bfloat16)
-                    fine = (volume - coarse.astype(jnp.float32)).astype(jnp.bfloat16)
-                    split[k * 2 * TX + r : k * 2 * TX + r + ROWS] = coarse
-                    split[k * 2 * TX + TX + r : k * 2 * TX + TX + r + ROWS] = fine
-            for n in range(2):
-                piece = jnp.dot(
-                    spread_x[...], split[:, n * 256 : (n + 1) * 256],
-                    preferred_element_type=jnp.float32,
-                )
-                if n == 0:
-                    edge_low[slot] = piece[:, :128]
-                    block[slot, :, :128] = piece[:, 128:]
-                else:
-                    block[slot, :, 128:] = piece[:, :128]
-                    edge_high[slot] = piece[:, 128:]
+            resample_x(z)
             start_y(slot)
+
+        @pl.when(slot == LAG_Y + 1)
+        def _():
+            gather_ramps()
 
         ready = slot - LAG_Y
 
@@ -246,16 +329,21 @@
 
             @pl.when(done == 0)
             def _():
-                inverse[...] = 1.0 / jnp.maximum(block[0, RX : RX + BX], 1.0)
-
-            @pl.when(done > 0)
-            def _():
-                block[done, RX : RX + BX] *= inverse[...]
-                store(done - 1).start()
+                invert()
+
+            out[done] = block[done, RX : RX + BX] * inverse[...]
 
         return carry
 
     lax.fori_loop(1, SLOTS + LAG_X, step, 0)
+
+    for present, copy in (
+        (has_low, ramps_low), (has_high, ramps_high),
+        (has_left, ramps_left), (has_right, ramps_right),
+    ):
+        @pl.when(present)
+        def _(copy=copy):
+            copy().wait_send()
 
     def finish(slot, carry):
         @pl.when(has_low)
@@ -273,10 +361,6 @@
         @pl.when(has_right)
         def _():
             to_right(slot).wait_send()
-
-        @pl.when(slot < NZ)
-        def _():
-            store(slot).wait()
 
         return carry
 
@@ -289,9 +373,9 @@
     dma = pltpu.SemaphoreType.DMA
     return pl.pallas_call(
         kernel,
-        out_shape=jax.ShapeDtypeStruct((NZ, BX, BY), jnp.float32),
+        out_shape=pltpu.VMEM((NZ, BX, BY), jnp.float32),
         in_specs=[hbm, smem, smem, smem],
-        out_specs=hbm,
+        out_specs=pl.BlockSpec(memory_space=pltpu.VMEM),
         scratch_shapes=[
             pltpu.VMEM((CAP, NZ, TX, TY), jnp.bfloat16),
             pltpu.VMEM((SLOTS, WX, RY), jnp.float32),
@@ -306,12 +390,18 @@
             pltpu.VMEM((CAP, TY, WY), jnp.bfloat16),
             pltpu.VMEM((WX, CAP * 2 * TX), jnp.bfloat16),
             pltpu.VMEM((BX, BY), jnp.float32),
-            dma((NZ,)), dma((NZ,)),
+            pltpu.VMEM((8, WX + WY), jnp.float32),
+            pltpu.VMEM((8, WX + WY), jnp.float32),
+            pltpu.VMEM((8, WX + WY), jnp.float32),
+            pltpu.VMEM((24, WX + BY), jnp.float32),
+            pltpu.VMEM((24, WX + BY), jnp.float32),
+            pltpu.VMEM((24, WX + BY), jnp.float32),
+            dma((NZ,)), dma((8,)),
             dma((SLOTS,)), dma((SLOTS,)), dma((SLOTS,)), dma((SLOTS,)),
             dma((SLOTS,)), dma((SLOTS,)), dma((SLOTS,)), dma((SLOTS,)),
         ],
         compiler_params=pltpu.CompilerParams(
-            collective_id=0, has_side_effects=True, vmem_limit_bytes=62 * 1024 * 1024,
+            collective_id=0, has_side_effects=True, vmem_limit_bytes=54 * 1024 * 1024,
         ),
     )(source_tiles, tile_offsets, tile_shifts, tile_counts)
 

time: 82.7 us -> 64.3 us (0.78)
  Pallas kernels: 77.1 us -> 61.5 us
  local copies, waits for them, and re-layouts: 4.66 us -> 2.02 us
    pallas_call x1, Pallas kernels: 77.1 us -> 61.5 us  [local(): pl.pallas_call(kernel, out_shape=pltpu.VMEM((NZ, BX, BY), jnp.float32), i...]
    unnamed x1, local copies, waits for them, and re-layouts: 4.66 us -> 2.02 us
where the time goes in v1:
time: 64.3 us; the launch traced here: 64.1 us
  Pallas kernels  61.5 us (96%)
  local copies, waits for them, and re-layouts  2.02 us (3%)
  between operations  0.66 us (1%)
    pallas_call x1, Pallas kernels, local(): pl.pallas_call(kernel, out_shape=pltpu.VMEM((NZ, BX, BY), jnp.float32), i...  61.5 us
    unnamed x1, local copies, waits for them, and re-layouts  2.02 us

profile of v1, /device:TPU:15, one launch (start us, length us, event | category | flops | bytes accessed | tf_op | source)
XLA Modules:
  0.0 64.1 jit_solution(10174429903258938289)
XLA Ops:
  0.7 61.5 %shard_map.46 = f32[32,128,256]{2,1,0:T(8,128)S(1)} custom-call(bf16[3,32,192,384]{3,2,1,0:T(8,128)(2,1)} %tiles.1, s32[2,3]{1,0:T(2,128)} %offsets.1, s32[3]{0:T(128)} %shifts.1, s32[1]{0:T(128)S(6)} %copy.7.counts), custom_call_target="tpu_custom_call" | custom-call | tf_op jit(solution)/shard_map/pallas_call | solution.py:374
  62.1 2.0 %copy.6 = f32[32,128,256]{2,1,0:T(8,128)} copy(f32[32,128,256]{2,1,0:T(8,128)S(1)} %shard_map.46) | data formatting | bytes 8388608
